TPU v7x, 512 devices: a whole 4x8x8 slice. The times are simulated.
512 devices in a mesh: clip: 8 (over z_hi, x), seq: 64 (over y, z_lo, core).
Axes of the slice: x: 4, y: 8, z: 8 (z_hi: 2, z_lo: 4; z = z_hi * 4 + z_lo), core: 2. Of those that a mesh axis runs over, the one named last changes fastest.
Arguments:
- spatial_saved: bfloat16 [3, 512, 256, 576], P(None, ('clip', 'seq')), parts along dimension 1, may hold values from -48 to 48
- hidden: bfloat16 [512, 256, 1152], P(('clip', 'seq')), parts along dimension 0, may hold values from -6 to 6
- temporal_out_grad: bfloat16 [512, 256, 576], P(('clip', 'seq')), parts along dimension 0, may hold values from -6 to 6
- stream_grad: bfloat16 [512, 256, 1152], P(('clip', 'seq')), parts along dimension 0, may hold values from -6 to 6
- modulation: float32 [1152], replicated, may hold values from -0.5 to 1
- temporal_weights: bfloat16 [1152, 1728], P('seq'), may hold values from -0.1875 to 0.1875
- spatial_weights: bfloat16 [576, 1152], P('seq'), may hold values from -0.25 to 0.25
Outputs:
- hidden_grad: bfloat16 [512, 256, 1152], P(('clip', 'seq')), parts along dimension 0
- spatial_grad: bfloat16 [3, 512, 256, 576], P(None, ('clip', 'seq')), parts along dimension 1
There are 8 independent parts, one for each index of `clip`. A program takes and returns all parts, laid end to end along the dimension named above; an argument that names none is the same for every part. Nothing has to cross between parts.
All inputs are finite; a program needn't handle non-finite values.
Results may differ from a plain program's by a relative error of at most 0.024.
Values may be sent and summed in bfloat16 or wider, within the bound.
A program may use at most 64 MiB of HBM per device.

v0:
```python
import math
import jax
import jax.numpy as jnp
from jax import lax
from jax.sharding import PartitionSpec as P

HEADS = 8
HD = 72
epsilon = 1e-06


def attend_grad(query, keys, values, grad_o, form):
    key_form = form.replace("l", "m")
    scale = 1.0 / math.sqrt(query.shape[-1])
    scores = (
        jnp.einsum(
            form + "," + key_form + "->bhlm", query, keys, preferred_element_type=jnp.float32
        )
        * scale
    )
    attention = jax.nn.softmax(scores, axis=-1)
    rounded = attention.astype(jnp.bfloat16)
    output = jnp.einsum(
        "bhlm," + key_form + "->" + form, rounded, values, preferred_element_type=jnp.float32
    )
    delta = jnp.einsum(form + "," + form + "->bhl", grad_o.astype(jnp.float32), output)
    spread = jnp.einsum(
        form + "," + key_form + "->bhlm", grad_o, values, preferred_element_type=jnp.float32
    )
    dscore = (attention * (spread - delta[..., None])).astype(jnp.bfloat16)
    grad_query = jnp.einsum(
        "bhlm," + key_form + "->" + form, dscore, keys, preferred_element_type=jnp.float32
    )
    grad_keys = jnp.einsum(
        "bhlm," + form + "->" + key_form, dscore, query, preferred_element_type=jnp.float32
    )
    grad_values = jnp.einsum(
        "bhlm," + form + "->" + key_form, rounded, grad_o, preferred_element_type=jnp.float32
    )
    return (
        (grad_query * scale).astype(jnp.bfloat16),
        (grad_keys * scale).astype(jnp.bfloat16),
        grad_values.astype(jnp.bfloat16),
    )


def split_heads(block):
    return block.reshape(block.shape[:-1] + (HEADS, HD))


def merge_heads(block):
    return block.reshape(block.shape[:-2] + (HEADS * HD,))


def layer_norm(hidden, modulation):
    widened = hidden.astype(jnp.float32)
    mean_value = jnp.mean(widened, axis=-1, keepdims=True)
    centered = widened - mean_value
    inverse = lax.rsqrt(jnp.mean(centered * centered, axis=-1, keepdims=True) + epsilon)
    normal_form = centered * inverse
    normed = (normal_form * (1.0 + modulation)).astype(jnp.bfloat16)
    return (normed, normal_form, inverse)


def norm_back(grad_normed, normal_form, inverse, modulation):
    scaled = grad_normed * (1.0 + modulation)
    return inverse * (
        scaled
        - jnp.mean(scaled, axis=-1, keepdims=True)
        - normal_form * jnp.mean(scaled * normal_form, axis=-1, keepdims=True)
    )


def temporal_backward(projected, grad_patch):
    width = HEADS * HD
    grads = attend_grad(
        split_heads(projected[..., :width]),
        split_heads(projected[..., width : 2 * width]),
        split_heads(projected[..., 2 * width :]),
        split_heads(grad_patch),
        "lbhd",
    )
    return jnp.concatenate([merge_heads(gradient) for gradient in grads], axis=-1)


def shards(
    spatial_saved,
    hidden,
    temporal_out_grad,
    stream_grad,
    modulation,
    temporal_weights,
    spatial_weights,
):
    grad_patch = lax.all_to_all(temporal_out_grad, "seq", split_axis=1, concat_axis=0, tiled=True)
    normed, normal_form, inverse = layer_norm(hidden, modulation)
    projected = jnp.einsum(
        "fpd,dc->fpc",
        normed,
        lax.all_gather(temporal_weights, "seq", axis=0, tiled=True),
        preferred_element_type=jnp.float32,
    ).astype(jnp.bfloat16)
    projected_patch = lax.all_to_all(projected, "seq", split_axis=1, concat_axis=0, tiled=True)
    grads_patch = temporal_backward(projected_patch, grad_patch)
    projection_grads = lax.all_to_all(grads_patch, "seq", split_axis=0, concat_axis=1, tiled=True)
    branch = norm_back(
        jnp.einsum(
            "fpc,dc->fpd",
            projection_grads,
            lax.all_gather(temporal_weights, "seq", axis=0, tiled=True),
            preferred_element_type=jnp.float32,
        ),
        normal_form,
        inverse,
        modulation,
    ).astype(jnp.bfloat16)
    branch = lax.optimization_barrier(branch)
    hidden_grad = (stream_grad.astype(jnp.float32) + branch.astype(jnp.float32)).astype(
        jnp.bfloat16
    )
    attention_grad = jnp.einsum(
        "fpd,cd->fpc",
        hidden_grad,
        lax.all_gather(spatial_weights, "seq", axis=0, tiled=True),
        preferred_element_type=jnp.float32,
    ).astype(jnp.bfloat16)
    spatial = attend_grad(
        split_heads(spatial_saved[0]),
        split_heads(spatial_saved[1]),
        split_heads(spatial_saved[2]),
        split_heads(attention_grad),
        "blhd",
    )
    spatial_grad = jnp.stack([merge_heads(gradient) for gradient in spatial])
    return (hidden_grad, spatial_grad)


def solution(mesh):
    return jax.shard_map(
        shards,
        mesh=mesh,
        in_specs=(
            P(None, ("clip", "seq"), None, None),
            P(("clip", "seq"), None, None),
            P(("clip", "seq"), None, None),
            P(("clip", "seq"), None, None),
            P(),
            P("seq", None),
            P("seq", None),
        ),
        out_specs=(P(("clip", "seq"), None, None), P(None, ("clip", "seq"), None, None)),
        check_vma=False,
    )
```

profile of v0, /device:TPU:1, one launch (start us, length us, event | category | flops | bytes accessed | tf_op | source)
XLA Modules:
  0.0 332.2 jit_solution(14576115687310509611)
XLA Ops:
  9.9 2.7 reduce.18
  13.7 15.3 %all-to-all-start.1 = ((bf16[64,2,1152]{2,1,0:T(2,128)(2,1)}), bf16[64,2,1152]{2,1,0:T(2,128)(2,1)}, u32[]{:S(2)}, u32[]{:S(2)}) async-start(bf16[64,2,1152]{2,1,0:T(2,128)(2,1)} %reshape.205), calls=%async_computation.1 | async-start | bytes 589824 | tf_op jit(solution)/shard_map/all_to_all | solution.py:95
  29.5 108.3 %all-gather.5.cloned.1.call-done = bf16[64,18,1728]{2,1,0:T(8,128)(2,1)} async-done(((bf16[1,18,1728]{2,1,0:T(8,128)(2,1)}), bf16[64,18,1728]{2,1,0:T(8,128)(2,1)}) %all-gather.5.cloned.1.call-update) | async-done | bytes 3981328 | tf_op jit(solution)/shard_map/all_gather | solution.py:100
  137.8 7.7 %reshape.189 = bf16[1152,1728]{1,0:T(8,128)(2,1)} reshape(bf16[64,18,1728]{2,1,0:T(8,128)(2,1)} %all-gather.5.cloned.1.call-done) | data formatting | bytes 7962624
  145.5 4.0 %fusion.2 = bf16[1,256,1728]{1,2,0:T(8,128)(2,1)S(1)} fusion(bf16[1152,1728]{1,0:T(8,128)(2,1)} %reshape.189, bf16[1,256,1152]{2,1,0:T(8,128)(2,1)S(1)} %copy-done, f32[1152]{0:T(1024)S(1)} %broadcast_add_fusion, f32[256]{0:T(256)S(1)} %add_rsqrt_fusion, f32[256]{0:T(256)S(1)} %broadcast_multiply_fusion.2), kind=kOutput, calls=%fused_computation.4 | convolution fusion | flops 1021132800 | bytes 5462528 | tf_op jit(solution)/shard_map/fpd,dc->fpc/dot_general | solution.py:97
  149.5 2.8 copy.37
  152.4 6.5 %reduce.17 = bf16[256,1728]{1,0:T(8,128)(2,1)S(1)} reduce(bf16[256,1,1728]{2,1,0:T(2,128)(2,1)S(1)} %bitcast.102, bf16[]{:T(256)} %broadcast.92), dimensions={1}, to_apply=%bitcast.78.reduce_sub_computation | reduce | bytes 1769474
  158.8 1.9 reshape.203
  160.8 7.6 %all-to-all-start = ((bf16[64,2,3456]{2,1,0:T(2,128)(2,1)}), bf16[64,2,3456]{2,1,0:T(2,128)(2,1)S(1)}, u32[]{:S(2)}, u32[]{:S(2)}) async-start(bf16[64,2,3456]{2,1,0:T(2,128)(2,1)} %reshape.203), calls=%async_computation | async-start | bytes 1769472 | tf_op jit(solution)/shard_map/all_to_all | solution.py:103
  168.4 10.9 %all-gather.7.cloned.1.call-start = ((), (), s32[]{:S(2)}) async-start(), calls=%async_computation.4 | async-start | bytes 2396160 | tf_op jit(solution)/shard_map/all_gather | solution.py:124
  179.4 2.5 reshape.206
  181.9 1.8 bitcast_reduce_fusion.1
  185.1 8.2 %all-to-all-done = bf16[64,2,3456]{2,1,0:T(2,128)(2,1)S(1)} async-done(((bf16[64,2,3456]{2,1,0:T(2,128)(2,1)}), bf16[64,2,3456]{2,1,0:T(2,128)(2,1)S(1)}, u32[]{:S(2)}, u32[]{:S(2)}) %all-to-all-start) | async-done | bytes 884768 | tf_op jit(solution)/shard_map/all_to_all | solution.py:103
  194.8 5.1 %bitcast_reduce_fusion = bf16[256,1728]{1,0:T(8,128)(2,1)S(1)} fusion(bf16[256,1,1728]{2,1,0:T(2,128)(2,1)S(1)} %reshape.204), kind=kLoop, calls=%fused_computation.80 | loop fusion | bytes 1769472 | tf_op jit(solution)/shard_map/all_to_all | solution.py:103
  204.0 1.7 convolution_bitcast_fusion
  206.6 1.7 fusion.13
  210.5 1.7 fusion.18
  213.4 1.7 copy.55
  215.1 6.2 %all-to-all-start.2 = ((bf16[64,4,1728]{2,1,0:T(4,128)(2,1)}), bf16[64,4,1728]{2,1,0:T(4,128)(2,1)S(1)}, u32[]{:S(2)}, u32[]{:S(2)}) async-start(bf16[64,4,1728]{2,1,0:T(4,128)(2,1)} %copy.55), calls=%async_computation.2 | async-start | bytes 1835008 | tf_op jit(solution)/shard_map/all_to_all | solution.py:105
  222.0 2.2 fusion.67
  224.2 1.8 fusion.29
  226.0 83.0 %all-gather.7.cloned.1.call-done = bf16[64,9,1152]{2,1,0:T(8,128)(2,1)} async-done(((bf16[1,9,1152]{2,1,0:T(8,128)(2,1)}), bf16[64,9,1152]{2,1,0:T(8,128)(2,1)}) %all-gather.7.cloned.1.call-update) | async-done | bytes 1327120 | tf_op jit(solution)/shard_map/all_gather | solution.py:124
  309.0 3.7 %reshape.191 = bf16[576,1152]{1,0:T(8,128)(2,1)} reshape(bf16[64,9,1152]{2,1,0:T(8,128)(2,1)} %all-gather.7.cloned.1.call-done) | data formatting | bytes 2654208
  314.1 3.9 %fusion.23 = (f32[256]{0:T(256)S(1)}, f32[256,1152]{1,0:T(8,128)S(1)}) fusion(bf16[1,256,1152]{2,1,0:T(8,128)(2,1)S(1)} %copy-done, f32[256]{0:T(256)S(1)} %add_rsqrt_fusion, f32[256]{0:T(256)S(1)} %broadcast_multiply_fusion.2, f32[1152]{0:T(1024)S(1)} %broadcast_add_fusion, bf16[256,1728]{1,0:T(8,128)(2,1)} %reshape.181, bf16[1152,1728]{1,0:T(8,128)(2,1)} %reshape.189), kind=kOutput, calls=%fused_computation.41 | convolution fusion | flops 1020985088 | bytes 6643200 | tf_op jit(solution)/shard_map/fpc,dc->fpd/dot_general | solution.py:107
  (63 shorter events, 24.4 us)
Async XLA Ops:
  7.2 130.7 %all-gather.5.cloned.1.call-start = ((), (), s32[]{:S(2)}) async-start(), calls=%async_computation.3 | async-start | bytes 5591040 | tf_op jit(solution)/shard_map/all_gather | solution.py:100
  9.3 19.7 %copy-start = (bf16[1,256,1152]{2,1,0:T(8,128)(2,1)S(1)}, bf16[1,256,1152]{2,1,0:T(8,128)(2,1)}, u32[]{:S(2)}) copy-start(bf16[1,256,1152]{2,1,0:T(8,128)(2,1)} %param.8) | copy-start | bytes 1769476
  12.6 16.9 %copy-start.8 = (f32[1152]{0:T(1024)S(1)}, f32[1152]{0:T(1024)}, u32[]{:S(2)}) copy-start(f32[1152]{0:T(1024)} %param.11) | copy-start | bytes 13828
  13.7 147.1 %all-to-all-start.1 = ((bf16[64,2,1152]{2,1,0:T(2,128)(2,1)}), bf16[64,2,1152]{2,1,0:T(2,128)(2,1)}, u32[]{:S(2)}, u32[]{:S(2)}) async-start(bf16[64,2,1152]{2,1,0:T(2,128)(2,1)} %reshape.205), calls=%async_computation.1 | async-start | bytes 589824 | tf_op jit(solution)/shard_map/all_to_all | solution.py:95
  160.8 32.6 %all-to-all-start = ((bf16[64,2,3456]{2,1,0:T(2,128)(2,1)}), bf16[64,2,3456]{2,1,0:T(2,128)(2,1)S(1)}, u32[]{:S(2)}, u32[]{:S(2)}) async-start(bf16[64,2,3456]{2,1,0:T(2,128)(2,1)} %reshape.203), calls=%async_computation | async-start | bytes 1769472 | tf_op jit(solution)/shard_map/all_to_all | solution.py:103
  168.4 140.6 %all-gather.7.cloned.1.call-start = ((), (), s32[]{:S(2)}) async-start(), calls=%async_computation.4 | async-start | bytes 2396160 | tf_op jit(solution)/shard_map/all_gather | solution.py:124
  204.0 1.7 copy-start.2
  215.1 6.2 %copy-start.5 = (bf16[3,1,256,576]{2,3,1,0:T(8,128)(2,1)S(1)}, bf16[3,1,256,576]{2,3,1,0:T(8,128)(2,1)}, u32[]{:S(2)}) copy-start(bf16[3,1,256,576]{2,3,1,0:T(8,128)(2,1)} %param.7) | copy-start | bytes 2654212
  215.1 97.7 %all-to-all-start.2 = ((bf16[64,4,1728]{2,1,0:T(4,128)(2,1)}), bf16[64,4,1728]{2,1,0:T(4,128)(2,1)S(1)}, u32[]{:S(2)}, u32[]{:S(2)}) async-start(bf16[64,4,1728]{2,1,0:T(4,128)(2,1)} %copy.55), calls=%async_computation.2 | async-start | bytes 1835008 | tf_op jit(solution)/shard_map/all_to_all | solution.py:105
  318.2 1.1 copy-start.6
  319.2 1.3 copy-start.3
  319.2 1.9 copy-start.4
  320.6 0.9 copy-start.7
  320.6 1.8 copy-start.1
Sparse Core Ops, SparseCore 0:
  10.1 127.6 all-gather.4
  179.5 129.4 all-gather.6
where the time goes:
time: 336 us; the launch traced here: 332 us
  waiting for transfers between devices  200 us (60%)
  local copies, waits for them, and re-layouts  43.1 us (13%)
  starting transfers between devices  40.1 us (12%)
  matrix products  20.2 us (6%)
  between operations  14.6 us (4%)
  other arithmetic  13.9 us (4%)
    all_gather x1, waiting for transfers between devices, shards(): lax.all_gather(temporal_weights, 'seq', axis=0, tiled=True)  108 us
    all_gather x1, waiting for transfers between devices, shards(): lax.all_gather(spatial_weights, 'seq', axis=0, tiled=True)  83 us
    unnamed x26, local copies, waits for them, and re-layouts  23.1 us
    all_to_all x1, starting transfers between devices, shards(): lax.all_to_all(temporal_out_grad, 'seq', split_axis=1, concat_axis=0, til...  15.3 us
    all_gather x1, starting transfers between devices, shards(): lax.all_gather(spatial_weights, 'seq', axis=0, tiled=True)  10.9 us
    unnamed x3, other arithmetic  9.99 us
    all_to_all x1, waiting for transfers between devices, shards(): lax.all_to_all(projected, 'seq', split_axis=1, concat_axis=0, tiled=True)  8.25 us
    all_to_all x1, starting transfers between devices, shards(): lax.all_to_all(projected, 'seq', split_axis=1, concat_axis=0, tiled=True)  7.62 us
  transfers between devices with their start and end apart: 5, of which 3 were waited for; matrix products, arithmetic and copies ran while one was open for 19% of the time, Pallas kernels for 0%

commit v1 on v0

--- a/solution.py
+++ b/solution.py
@@ -97,7 +97,10 @@
     projected = jnp.einsum(
         "fpd,dc->fpc",
         normed,
-        lax.all_gather(temporal_weights, "seq", axis=0, tiled=True),
+        jnp.concatenate(
+            lax.all_to_all(jnp.stack([temporal_weights] * lax.axis_size("seq")), "seq", 0, 0),
+            axis=0,
+        ),
         preferred_element_type=jnp.float32,
     ).astype(jnp.bfloat16)
     projected_patch = lax.all_to_all(projected, "seq", split_axis=1, concat_axis=0, tiled=True)

time: 336 us -> 410 us (1.22)
  waiting for transfers between devices: 200 us -> 251 us
  local copies, waits for them, and re-layouts: 43.1 us -> 53.8 us
  starting transfers between devices: 40.1 us -> 50.3 us
    all_to_all x0 -> x1, waiting for transfers between devices: none -> 123 us  [shards(): lax.all_to_all(jnp.stack([temporal_weights] * lax.axis_size('seq')), 'seq...]
    all_gather x1, waiting for transfers between devices: 83 us -> 0.02 us  [shards(): lax.all_gather(spatial_weights, 'seq', axis=0, tiled=True)]
    all_to_all x0 -> x1, starting transfers between devices: none -> 14.9 us  [shards(): lax.all_to_all(jnp.stack([temporal_weights] * lax.axis_size('seq')), 'seq...]
    all_to_all x1, waiting for transfers between devices: 8.25 us -> 20.8 us  [shards(): lax.all_to_all(projected, 'seq', split_axis=1, concat_axis=0, tiled=True)]
    all_gather x1, starting transfers between devices: 10.9 us -> 0.04 us  [shards(): lax.all_gather(spatial_weights, 'seq', axis=0, tiled=True)]
    reshape x0 -> x1, local copies, waits for them, and re-layouts: none -> 7.75 us  [shards(): jnp.concatenate(lax.all_to_all(jnp.stack([temporal_weights] * lax.axis_si...]
    unnamed x26 -> x28, local copies, waits for them, and re-layouts: 23.1 us -> 22.5 us
  transfers between devices with their start and end apart: 5 -> 6, of which waited for: 3 -> 3; matrix products, arithmetic and copies ran while one was open for 19% -> 18% of each run, Pallas kernels for 0% -> 0%
where the time goes in v1:
time: 410 us; the launch traced here: 404 us
  waiting for transfers between devices  251 us (61%)
  local copies, waits for them, and re-layouts  53.8 us (13%)
  starting transfers between devices  50.3 us (12%)
  matrix products  20.2 us (5%)
  between operations  14.6 us (4%)
  other arithmetic  13.9 us (3%)
    all_to_all x1, waiting for transfers between devices, shards(): lax.all_to_all(jnp.stack([temporal_weights] * lax.axis_size('seq')), 'seq...  123 us
    all_gather x1, waiting for transfers between devices, shards(): lax.all_gather(temporal_weights, 'seq', axis=0, tiled=True)  106 us
    unnamed x28, local copies, waits for them, and re-layouts  22.5 us
    all_to_all x1, waiting for transfers between devices, shards(): lax.all_to_all(projected, 'seq', split_axis=1, concat_axis=0, tiled=True)  20.8 us
    all_to_all x1, starting transfers between devices, shards(): lax.all_to_all(temporal_out_grad, 'seq', split_axis=1, concat_axis=0, til...  18.8 us
    all_to_all x1, starting transfers between devices, shards(): lax.all_to_all(jnp.stack([temporal_weights] * lax.axis_size('seq')), 'seq...  14.9 us
    all_to_all x1, starting transfers between devices, shards(): lax.all_to_all(projected, 'seq', split_axis=1, concat_axis=0, tiled=True)  10.6 us
    unnamed x3, other arithmetic  10 us
  transfers between devices with their start and end apart: 6, of which 3 were waited for; matrix products, arithmetic and copies ran while one was open for 18% of the time, Pallas kernels for 0%

profile of v1, /device:TPU:1, one launch (start us, length us, event | category | flops | bytes accessed | tf_op | source)
XLA Modules:
  0.0 404.3 jit_solution(5011394023485326789)
XLA Ops:
  7.2 3.6 stack.4
  10.8 14.9 %all-to-all-start = ((bf16[64,18,1728]{2,1,0:T(8,128)(2,1)}), bf16[64,18,1728]{2,1,0:T(8,128)(2,1)}, u32[]{:S(2)}, u32[]{:S(2)}) async-start(bf16[64,18,1728]{2,1,0:T(8,128)(2,1)} %stack.4), calls=%async_computation | async-start | bytes 11010048 | tf_op jit(solution)/shard_map/all_to_all | solution.py:101
  28.3 2.7 reduce.18
  32.6 122.7 %all-to-all-done = bf16[64,18,1728]{2,1,0:T(8,128)(2,1)} async-done(((bf16[64,18,1728]{2,1,0:T(8,128)(2,1)}), bf16[64,18,1728]{2,1,0:T(8,128)(2,1)}, u32[]{:S(2)}, u32[]{:S(2)}) %all-to-all-start) | async-done | bytes 3981344 | tf_op jit(solution)/shard_map/all_to_all | solution.py:101
  155.3 18.8 %all-to-all-start.2 = ((bf16[64,2,1152]{2,1,0:T(2,128)(2,1)}), bf16[64,2,1152]{2,1,0:T(2,128)(2,1)}, u32[]{:S(2)}, u32[]{:S(2)}) async-start(bf16[64,2,1152]{2,1,0:T(2,128)(2,1)} %reshape.211), calls=%async_computation.2 | async-start | bytes 589824 | tf_op jit(solution)/shard_map/all_to_all | solution.py:95
  174.1 7.8 %reshape.179 = bf16[1152,1728]{1,0:T(8,128)(2,1)} reshape(bf16[64,18,1728]{2,1,0:T(8,128)(2,1)} %all-to-all-done) | data formatting | bytes 7962624 | tf_op jit(solution)/shard_map/reshape | solution.py:100
  181.8 4.0 fusion.2
  185.9 2.8 copy.37
  188.7 6.5 %reduce.17 = bf16[256,1728]{1,0:T(8,128)(2,1)S(1)} reduce(bf16[256,1,1728]{2,1,0:T(2,128)(2,1)S(1)} %bitcast.102, bf16[]{:T(256)} %broadcast.94), dimensions={1}, to_apply=%bitcast.78.reduce_sub_computation | reduce | bytes 1769474
  195.1 1.9 reshape.209
  197.1 10.6 %all-to-all-start.1 = ((bf16[64,2,3456]{2,1,0:T(2,128)(2,1)}), bf16[64,2,3456]{2,1,0:T(2,128)(2,1)S(1)}, u32[]{:S(2)}, u32[]{:S(2)}) async-start(bf16[64,2,3456]{2,1,0:T(2,128)(2,1)} %reshape.209), calls=%async_computation.1 | async-start | bytes 1769472 | tf_op jit(solution)/shard_map/all_to_all | solution.py:106
  207.7 2.5 reshape.212
  210.2 1.8 bitcast_reduce_fusion.1
  213.4 20.8 %all-to-all-done.1 = bf16[64,2,3456]{2,1,0:T(2,128)(2,1)S(1)} async-done(((bf16[64,2,3456]{2,1,0:T(2,128)(2,1)}), bf16[64,2,3456]{2,1,0:T(2,128)(2,1)S(1)}, u32[]{:S(2)}, u32[]{:S(2)}) %all-to-all-start.1) | async-done | bytes 884768 | tf_op jit(solution)/shard_map/all_to_all | solution.py:106
  235.9 5.1 %bitcast_reduce_fusion = bf16[256,1728]{1,0:T(8,128)(2,1)S(1)} fusion(bf16[256,1,1728]{2,1,0:T(2,128)(2,1)S(1)} %reshape.210), kind=kLoop, calls=%fused_computation.80 | loop fusion | bytes 1769472 | tf_op jit(solution)/shard_map/all_to_all | solution.py:106
  247.6 1.7 fusion.13
  251.5 1.7 fusion.18
  256.2 6.0 %all-to-all-start.3 = ((bf16[64,4,1728]{2,1,0:T(4,128)(2,1)}), bf16[64,4,1728]{2,1,0:T(4,128)(2,1)S(1)}, u32[]{:S(2)}, u32[]{:S(2)}) async-start(bf16[64,4,1728]{2,1,0:T(4,128)(2,1)} %copy.55), calls=%async_computation.3 | async-start | bytes 1835008 | tf_op jit(solution)/shard_map/all_to_all | solution.py:108
  263.0 2.1 fusion.67
  265.1 1.8 fusion.29
  266.9 3.7 reshape.197
  270.7 106.4 %all-gather.5.cloned.1.call-done = bf16[64,18,1728]{2,1,0:T(8,128)(2,1)} async-done(((bf16[1,18,1728]{2,1,0:T(8,128)(2,1)}), bf16[64,18,1728]{2,1,0:T(8,128)(2,1)}) %all-gather.5.cloned.1.call-update) | async-done | bytes 3981328 | tf_op jit(solution)/shard_map/all_gather | solution.py:113
  377.1 7.7 %reshape.195 = bf16[1152,1728]{1,0:T(8,128)(2,1)} reshape(bf16[64,18,1728]{2,1,0:T(8,128)(2,1)} %all-gather.5.cloned.1.call-done) | data formatting | bytes 7962624
  386.2 3.9 fusion.23
  (69 shorter events, 27.9 us)
Async XLA Ops:
  10.8 16.4 %copy-start.8 = (bf16[1,256,576]{1,2,0:T(8,128)(2,1)S(1)}, bf16[1,256,576]{1,2,0:T(8,128)(2,1)}, u32[]{:S(2)}) copy-start(bf16[1,256,576]{1,2,0:T(8,128)(2,1)} %param.9) | copy-start | bytes 884740
  10.8 144.5 %all-to-all-start = ((bf16[64,18,1728]{2,1,0:T(8,128)(2,1)}), bf16[64,18,1728]{2,1,0:T(8,128)(2,1)}, u32[]{:S(2)}, u32[]{:S(2)}) async-start(bf16[64,18,1728]{2,1,0:T(8,128)(2,1)} %stack.4), calls=%async_computation | async-start | bytes 11010048 | tf_op jit(solution)/shard_map/all_to_all | solution.py:101
  25.6 241.3 %all-gather.7.cloned.1.call-start = ((), (), s32[]{:S(2)}) async-start(), calls=%async_computation.5 | async-start | bytes 2396160 | tf_op jit(solution)/shard_map/all_gather | solution.py:127
  26.4 5.7 %copy-start = (bf16[1,256,1152]{2,1,0:T(8,128)(2,1)S(1)}, bf16[1,256,1152]{2,1,0:T(8,128)(2,1)}, u32[]{:S(2)}) copy-start(bf16[1,256,1152]{2,1,0:T(8,128)(2,1)} %param.8) | copy-start | bytes 1769476
  26.4 350.7 %all-gather.5.cloned.1.call-start = ((), (), s32[]{:S(2)}) async-start(), calls=%async_computation.4 | async-start | bytes 5591040 | tf_op jit(solution)/shard_map/all_gather | solution.py:113
  28.3 4.3 %copy-start.9 = (f32[1152]{0:T(1024)S(1)}, f32[1152]{0:T(1024)}, u32[]{:S(2)}) copy-start(f32[1152]{0:T(1024)} %param.11) | copy-start | bytes 13828
  155.3 41.8 %all-to-all-start.2 = ((bf16[64,2,1152]{2,1,0:T(2,128)(2,1)}), bf16[64,2,1152]{2,1,0:T(2,128)(2,1)}, u32[]{:S(2)}, u32[]{:S(2)}) async-start(bf16[64,2,1152]{2,1,0:T(2,128)(2,1)} %reshape.211), calls=%async_computation.2 | async-start | bytes 589824 | tf_op jit(solution)/shard_map/all_to_all | solution.py:95
  197.1 37.1 %all-to-all-start.1 = ((bf16[64,2,3456]{2,1,0:T(2,128)(2,1)}), bf16[64,2,3456]{2,1,0:T(2,128)(2,1)S(1)}, u32[]{:S(2)}, u32[]{:S(2)}) async-start(bf16[64,2,3456]{2,1,0:T(2,128)(2,1)} %reshape.209), calls=%async_computation.1 | async-start | bytes 1769472 | tf_op jit(solution)/shard_map/all_to_all | solution.py:106
  245.0 1.7 copy-start.2
  256.2 6.0 %copy-start.5 = (bf16[3,1,256,576]{2,3,1,0:T(8,128)(2,1)S(1)}, bf16[3,1,256,576]{2,3,1,0:T(8,128)(2,1)}, u32[]{:S(2)}) copy-start(bf16[3,1,256,576]{2,3,1,0:T(8,128)(2,1)} %param.7) | copy-start | bytes 2654212
  256.2 128.7 %all-to-all-start.3 = ((bf16[64,4,1728]{2,1,0:T(4,128)(2,1)}), bf16[64,4,1728]{2,1,0:T(4,128)(2,1)S(1)}, u32[]{:S(2)}, u32[]{:S(2)}) async-start(bf16[64,4,1728]{2,1,0:T(4,128)(2,1)} %copy.55), calls=%async_computation.3 | async-start | bytes 1835008 | tf_op jit(solution)/shard_map/all_to_all | solution.py:108
  390.3 1.1 copy-start.6
  391.3 1.3 copy-start.3
  391.3 1.9 copy-start.4
  392.7 0.9 copy-start.7
  392.7 1.8 copy-start.1
Sparse Core Ops, SparseCore 0:
  28.6 211.5 all-gather.6
  242.4 134.6 all-gather.4
